TPU v7x, 32 devices: a whole 2x2x4 slice. The times are simulated.
32 devices in a mesh: blk: 8 (over z, x), ga: 4 (over y, core).
Axes of the slice: x: 2, y: 2, z: 4, core: 2. Of those that a mesh axis runs over, the one named last changes fastest.
Arguments:
- pair_val: bfloat16 [16, 16, 16, 2048], P('blk', None, None, 'ga'), may hold values from -0.125 to 0.125
- pair_con: bfloat16 [16, 16, 16, 2048], P('blk', None, None, 'ga'), may hold values from -6 to 6
- screened: bfloat16 [16, 2048, 2048], P('blk', None, 'ga'), may hold values from -0.125 to 0.125
- amplitude: bfloat16 [16, 16], P('blk'), may hold values from -6 to 6
- qmap: int32 [16, 16], P('blk'), may hold values from 0 to 15, as said below
Outputs:
- kernel_x: float32 [16, 16], P('blk')
Inputs may be any that keep to these rules, and one draw needn't show every extreme that they name: qmap[k, k'] is the label of the difference k - k' (periodic) on a grid of 8 by 2 points, with the points and the differences labelled at random; every row and every column holds each label once.
All inputs are finite; a program needn't handle non-finite values.
Results may differ from a plain program's by a relative error of at most 0.004.
Values may be sent and summed in bfloat16 or wider, within the bound.
No kernel may reach another device: no remote copies, remote signals or barrier semaphores. Data moves between devices by JAX's collectives and lax.ppermute only.
A program may use at most 64 MiB of HBM per device.

v0:
```python
import jax
import jax.numpy as jnp
from jax import lax
from jax.sharding import PartitionSpec as P

NV = 4
NC = 4


def inverse_rows(qmap):
    total = qmap.shape[1]
    labels = jnp.arange(total, dtype=jnp.int32)
    hits = (qmap[:, :, None] == labels[None, None, :]).astype(jnp.int32)
    return jnp.sum(hits * labels[None, :, None], axis=1)


def swap(value, axis, size, step):
    return lax.ppermute(value, axis, [(i, i ^ step) for i in range(size)])


def body_of(blk, ga):

    def body(pair_val, pair_con, screened, amplitude, qmap):
        local_k, total, band_pairs, width = pair_val.shape
        local_q = screened.shape[0]
        slot = lax.axis_index("ga")
        every_amp = lax.all_gather(amplitude, "blk", axis=0, tiled=True)
        partner = inverse_rows(qmap)
        con_sorted = jnp.take_along_axis(pair_con, partner[:, :, None, None], axis=1)
        con_sorted, every_amp = lax.optimization_barrier((con_sorted, every_amp))
        con_in = lax.all_to_all(con_sorted, "blk", split_axis=1, concat_axis=0, tiled=True)
        val_sorted = jnp.take_along_axis(pair_val, partner[:, :, None, None], axis=1)
        amp_sorted = every_amp[partner].reshape(local_k, total, NV, NC)
        val_five = val_sorted.reshape(local_k, total, NV, NV, width)
        zeta = jnp.einsum(
            "kqavg,kqvc->kqacg", val_five, amp_sorted, preferred_element_type=jnp.float32
        )
        zeta = zeta.astype(jnp.bfloat16).reshape(local_k, total, NV * NC, width)
        far = swap(con_in, "ga", ga, ga // 2)
        near = swap(con_in, "ga", ga, 1)
        zeta_in = lax.all_to_all(zeta, "blk", split_axis=1, concat_axis=0, tiled=True)
        pieces = {0: con_in, 1: near, ga // 2: far, ga // 2 + 1: swap(far, "ga", ga, 1)}
        weights = screened.reshape(local_q, ga, width, screened.shape[2])
        unit = 0.0
        for key, held in pieces.items():
            block = lax.dynamic_index_in_dim(weights, slot ^ key, 1, keepdims=False)
            unit = unit + jnp.einsum(
                "kqxg,qgh->kqxh", held, block, preferred_element_type=jnp.float32
            )
        unit = unit.astype(jnp.bfloat16).reshape(total, local_q, NC, NC, -1)
        zeta = zeta_in.reshape(total, local_q, NV, NC, -1)
        terms = jnp.einsum("kqcyg,kqayg->kac", unit, zeta, preferred_element_type=jnp.float32)
        terms = terms.reshape(blk, 1, local_k, NV * NC)
        terms = jnp.broadcast_to(terms, (blk, ga, local_k, NV * NC)).reshape(
            blk * ga, local_k, NV * NC
        )
        back = lax.all_to_all(terms, ("blk", "ga"), split_axis=0, concat_axis=0, tiled=True)
        return jnp.sum(back, 0) / total

    return body


def solution(mesh):
    placed = (
        P("blk", None, None, "ga"),
        P("blk", None, None, "ga"),
        P("blk", None, "ga"),
        P("blk", None),
        P("blk", None),
    )
    return jax.shard_map(
        body_of(mesh.shape["blk"], mesh.shape["ga"]),
        mesh=mesh,
        in_specs=placed,
        out_specs=P("blk", None),
        check_vma=False,
    )
```

profile of v0, /device:TPU:0, one launch (start us, length us, event | category | flops | bytes accessed | tf_op | source)
XLA Modules:
  0.0 74.7 jit_solution(2706167675406388047)
XLA Ops:
  0.0 0.0 copy-start
  0.0 0.8 %select_reduce_fusion = s32[2,16]{1,0:T(2,128)S(1)} fusion(s32[2,16]{1,0:T(2,128)} %param.11), kind=kLoop, calls=%fused_computation.24 | loop fusion | flops 1504 | bytes 256 | tf_op jit(solution)/shard_map/reduce_sum | solution.py:14
  0.9 0.1 reshape.99
  0.9 0.1 copy-done
  1.1 0.6 gather_fusion.2
  1.7 1.7 %gather_fusion.1 = bf16[32,16,512]{2,1,0:T(8,128)(2,1)S(1)} fusion(bf16[2,16,16,512]{3,2,1,0:T(8,128)(2,1)} %param.8, s32[32]{0:T(128)S(1)} %reshape.99), kind=kCustom, calls=%fused_computation.clone | custom fusion | bytes 1048832 | tf_op jit(solution)/shard_map/jit(take_along_axis)/gather | solution.py:29
  3.4 22.4 %all-gather = bf16[8,2,16]{2,1,0:T(2,128)(2,1)S(1)} all-gather(bf16[1,2,16]{2,1,0:T(2,128)(2,1)} %bitcast.98), channel_id=1, replica_groups=mesh['blk'=8,'ga'=4] {'blk'}, dimensions={0}, use_global_device_ids=true | all-gather | bytes 576 | tf_op jit(solution)/shard_map/all_gather | solution.py:27
  25.8 0.2 broadcast_select_fusion
  26.0 0.8 %copy.96 = bf16[2,16,16,512]{3,2,0,1:T(8,128)(2,1)} copy(bf16[2,16,16,512]{3,2,1,0:T(8,128)(2,1)S(1)} %get-tuple-element.9) | data formatting | bytes 1048576 | tf_op jit(solution)/shard_map/optimization_barrier | solution.py:30
  26.8 3.5 %all-to-all-start.1 = ((bf16[2,16,16,512]{3,2,0,1:T(8,128)(2,1)}), bf16[2,16,16,512]{3,2,0,1:T(8,128)(2,1)S(1)}, u32[]{:S(2)}, u32[]{:S(2)}) async-start(bf16[2,16,16,512]{3,2,0,1:T(8,128)(2,1)} %copy.96), calls=%async_computation.1 | async-start | bytes 1048576 | tf_op jit(solution)/shard_map/all_to_all | solution.py:31
  30.3 0.1 reshape.78
  30.4 0.6 gather_fusion
  31.0 0.1 copy.90
  31.1 0.1 reshape.56
  31.1 0.1 copy.107
  31.3 0.1 reshape.57
  31.4 0.4 fusion.2
  31.8 0.1 reshape.58
  32.0 0.8 %copy.92 = bf16[2,16,16,512]{3,2,0,1:T(8,128)(2,1)} copy(bf16[2,16,16,512]{3,2,1,0:T(8,128)(2,1)S(1)} %reshape.58) | data formatting | bytes 1048576 | tf_op jit(solution)/shard_map/reshape | solution.py:38
  32.8 8.4 %all-to-all-done.1 = bf16[2,16,16,512]{3,2,0,1:T(8,128)(2,1)S(1)} async-done(((bf16[2,16,16,512]{3,2,0,1:T(8,128)(2,1)}), bf16[2,16,16,512]{3,2,0,1:T(8,128)(2,1)S(1)}, u32[]{:S(2)}, u32[]{:S(2)}) %all-to-all-start.1) | async-done | bytes 524320 | tf_op jit(solution)/shard_map/all_to_all | solution.py:31
  41.2 3.7 %all-to-all-start = ((bf16[2,16,16,512]{3,2,0,1:T(8,128)(2,1)}), bf16[2,16,16,512]{3,2,0,1:T(8,128)(2,1)S(1)}, u32[]{:S(2)}, u32[]{:S(2)}) async-start(bf16[2,16,16,512]{3,2,0,1:T(8,128)(2,1)} %copy.92), calls=%async_computation | async-start | bytes 1048576 | tf_op jit(solution)/shard_map/all_to_all | solution.py:41
  45.0 1.6 %collective-permute-start.1 = (bf16[16,2,16,512]{3,2,0,1:T(8,128)(2,1)S(1)}, bf16[16,2,16,512]{3,2,0,1:T(8,128)(2,1)S(1)}, u32[]{:S(2)}, u32[]{:S(2)}) collective-permute-start(bf16[16,2,16,512]{3,2,0,1:T(8,128)(2,1)S(1)} %bitcast.92), channel_id=1, source_target_pairs={{0,2},{1,3},{2,0},{3,1},{4,6},{5,7},{6,4},{7,5},{8,10},{9,11},{10,... | collective-permute-start | bytes 1572872 | tf_op jit(solution)/shard_map/ppermute | solution.py:18
  46.5 0.0 collective-permute-start
  46.5 10.8 %all-to-all-done = bf16[2,16,16,512]{3,2,0,1:T(8,128)(2,1)S(1)} async-done(((bf16[2,16,16,512]{3,2,0,1:T(8,128)(2,1)}), bf16[2,16,16,512]{3,2,0,1:T(8,128)(2,1)S(1)}, u32[]{:S(2)}, u32[]{:S(2)}) %all-to-all-start) | async-done | bytes 524320 | tf_op jit(solution)/shard_map/all_to_all | solution.py:41
  57.3 0.5 copy.94
  57.9 0.0 copy-start.1
  57.9 1.8 %fusion.6 = f32[2,512,16,16]{1,3,2,0:T(8,128)S(1)} fusion(bf16[16,2,16,512]{3,2,0,1:T(8,128)(2,1)S(1)} %bitcast.94, bf16[2,4,512,512]{3,2,1,0:T(8,128)(2,1)} %bitcast.99, s32[]{:T(128)S(6)} %select_n.30), kind=kOutput, calls=%fused_computation.14 | convolution fusion | flops 268435456 | bytes 2621444 | tf_op jit(solution)/shard_map/kqxg,qgh->kqxh/dot_general | solution.py:47
  59.7 0.0 collective-permute-done.1
  59.7 0.1 collective-permute-start.2
  59.8 0.0 collective-permute-done
  59.8 0.6 copy-done.1
  60.4 0.4 convolution_add_fusion.2
  60.9 0.5 convolution_add_fusion.1
  61.3 0.4 collective-permute-done.2
  61.7 0.4 fusion.1
  62.2 0.1 reshape.61
  62.3 0.9 %convolution_bitcast_fusion = f32[16,4,4]{2,1,0:T(4,128)S(1)} fusion(bf16[16,2,4,4,512]{4,3,2,0,1:T(4,128)(2,1)S(1)} %reshape.61, bf16[16,2,4,4,512]{4,1,3,2,0:T(2,128)(2,1)S(1)} %bitcast.95), kind=kOutput, calls=%fused_computation.10 | convolution fusion | flops 2097152 | bytes 1049600 | tf_op jit(solution)/shard_map/kqcyg,kqayg->kac/dot_general | solution.py:52
  63.2 0.1 broadcast_in_dim.22
  63.3 10.8 %all_to_all.38 = f32[32,2,16]{2,1,0:T(2,128)S(1)} all-to-all(f32[32,2,16]{2,1,0:T(2,128)S(1)} %copy.105), channel_id=1, replica_groups=mesh['blk'=8,'ga'=4] {'blk','ga'}, dimensions={0} | all-to-all | bytes 8192 | tf_op jit(solution)/shard_map/all_to_all | solution.py:57
  74.2 0.6 broadcast_multiply_fusion
  (8 shorter events, 0.1 us)
Async XLA Ops:
  0.0 1.1 %copy-start = (bf16[2,16,16,512]{3,2,1,0:T(8,128)(2,1)S(1)}, bf16[2,16,16,512]{3,2,1,0:T(8,128)(2,1)}, u32[]{:S(2)}) copy-start(bf16[2,16,16,512]{3,2,1,0:T(8,128)(2,1)} %param.7) | copy-start | bytes 1572868
  26.8 14.4 %all-to-all-start.1 = ((bf16[2,16,16,512]{3,2,0,1:T(8,128)(2,1)}), bf16[2,16,16,512]{3,2,0,1:T(8,128)(2,1)S(1)}, u32[]{:S(2)}, u32[]{:S(2)}) async-start(bf16[2,16,16,512]{3,2,0,1:T(8,128)(2,1)} %copy.96), calls=%async_computation.1 | async-start | bytes 1048576 | tf_op jit(solution)/shard_map/all_to_all | solution.py:31
  41.2 16.1 %all-to-all-start = ((bf16[2,16,16,512]{3,2,0,1:T(8,128)(2,1)}), bf16[2,16,16,512]{3,2,0,1:T(8,128)(2,1)S(1)}, u32[]{:S(2)}, u32[]{:S(2)}) async-start(bf16[2,16,16,512]{3,2,0,1:T(8,128)(2,1)} %copy.92), calls=%async_computation | async-start | bytes 1048576 | tf_op jit(solution)/shard_map/all_to_all | solution.py:41
  45.0 14.8 %collective-permute-start.1 = (bf16[16,2,16,512]{3,2,0,1:T(8,128)(2,1)S(1)}, bf16[16,2,16,512]{3,2,0,1:T(8,128)(2,1)S(1)}, u32[]{:S(2)}, u32[]{:S(2)}) collective-permute-start(bf16[16,2,16,512]{3,2,0,1:T(8,128)(2,1)S(1)} %bitcast.92), channel_id=1, source_target_pairs={{0,2},{1,3},{2,0},{3,1},{4,6},{5,7},{6,4},{7,5},{8,10},{9,11},{10,... | collective-permute-start | bytes 1572872 | tf_op jit(solution)/shard_map/ppermute | solution.py:18
  46.5 13.3 %collective-permute-start = (bf16[16,2,16,512]{3,2,0,1:T(8,128)(2,1)S(1)}, bf16[16,2,16,512]{3,2,0,1:T(8,128)(2,1)S(1)}, u32[]{:S(2)}, u32[]{:S(2)}) collective-permute-start(bf16[16,2,16,512]{3,2,0,1:T(8,128)(2,1)S(1)} %bitcast.93), channel_id=1, source_target_pairs={{0,1},{1,0},{2,3},{3,2},{4,5},{5,4},{6,7},{7,6},{8,9},{9,8},{10,11... | collective-permute-start | bytes 1572872 | tf_op jit(solution)/shard_map/ppermute | solution.py:18
  57.9 2.5 %copy-start.1 = (bf16[2,2048,512]{2,1,0:T(8,128)(2,1)S(1)}, bf16[2,2048,512]{2,1,0:T(8,128)(2,1)}, u32[]{:S(2)}) copy-start(bf16[2,2048,512]{2,1,0:T(8,128)(2,1)} %param.9) | copy-start | bytes 12582916
  59.7 2.0 %collective-permute-start.2 = (bf16[16,2,16,512]{3,2,0,1:T(8,128)(2,1)S(1)}, bf16[16,2,16,512]{3,2,0,1:T(8,128)(2,1)S(1)}, u32[]{:S(2)}, u32[]{:S(2)}) collective-permute-start(bf16[16,2,16,512]{3,2,0,1:T(8,128)(2,1)S(1)} %collective-permute-done.1), channel_id=1, source_target_pairs={{0,1},{1,0},{2,3},{3,2},{4,5},{5,4},{6,7},{7,6},{8,9},{9,8},{10,11... | collective-permute-start | bytes 1572872 | tf_op jit(solution)/shard_map/ppermute | solution.py:18
where the time goes:
time: 75.1 us; the launch traced here: 74.7 us
  blocking collectives  33.2 us (44%)
  waiting for transfers between devices  19.6 us (26%)
  starting transfers between devices  8.84 us (12%)
  local copies, waits for them, and re-layouts  6.81 us (9%)
  matrix products  4.45 us (6%)
  other arithmetic  1.62 us (2%)
    all_gather x1, blocking collectives, body(): every_amp = lax.all_gather(amplitude, 'blk', axis=0, tiled=True)  22.4 us
    all_to_all x1, waiting for transfers between devices, body(): lax.all_to_all(zeta, 'blk', split_axis=1, concat_axis=0, tiled=True)  10.8 us
    all_to_all x1, blocking collectives, body(): lax.all_to_all(terms, ('blk', 'ga'), split_axis=0, concat_axis=0, tiled=T...  10.8 us
    all_to_all x1, waiting for transfers between devices, body(): lax.all_to_all(con_sorted, 'blk', split_axis=1, concat_axis=0, tiled=True)  8.4 us
    all_to_all x1, starting transfers between devices, body(): lax.all_to_all(zeta, 'blk', split_axis=1, concat_axis=0, tiled=True)  3.69 us
    all_to_all x1, starting transfers between devices, body(): lax.all_to_all(con_sorted, 'blk', split_axis=1, concat_axis=0, tiled=True)  3.49 us
    dot_general x4, matrix products, body(): jnp.einsum('kqxg,qgh->kqxh', held, block, preferred_element_type=jnp.floa...  3.15 us
    gather x2, local copies, waits for them, and re-layouts, body(): jnp.take_along_axis(pair_con, partner[:, :, None, None], axis=1)  1.75 us
  transfers between devices with their start and end apart: 5, of which 3 were waited for; matrix products, arithmetic and copies ran while one was open for 8% of the time, Pallas kernels for 0%

commit v1 on v0

--- a/solution.py
+++ b/solution.py
@@ -24,7 +24,14 @@
         local_k, total, band_pairs, width = pair_val.shape
         local_q = screened.shape[0]
         slot = lax.axis_index("ga")
-        every_amp = lax.all_gather(amplitude, "blk", axis=0, tiled=True)
+        ring = [amplitude]
+        for hop in range(7):
+            ring.append(lax.ppermute(ring[-1], "blk", [(dev, (dev + 1) % 8) for dev in range(8)]))
+        every_amp = jnp.roll(
+            jnp.concatenate(ring[::-1], axis=0),
+            (lax.axis_index("blk") + 1) * ring[0].shape[0],
+            axis=0,
+        )
         partner = inverse_rows(qmap)
         con_sorted = jnp.take_along_axis(pair_con, partner[:, :, None, None], axis=1)
         con_sorted, every_amp = lax.optimization_barrier((con_sorted, every_amp))

time: 75.1 us -> 96.1 us (1.28)
  waiting for transfers between devices: 19.6 us -> 56.3 us
  blocking collectives: 33.2 us -> 11.1 us
  starting transfers between devices: 8.84 us -> 15.3 us
    ppermute x0 -> x7, waiting for transfers between devices: none -> 38.8 us  [body(): lax.ppermute(ring[-1], 'blk', [(dev, (dev + 1) % 8) for dev in range(8)])]
    all_gather x1 -> x0, blocking collectives: 22.4 us -> none  [body(): every_amp = lax.all_gather(amplitude, 'blk', axis=0, tiled=True)]
    ppermute x0 -> x7, starting transfers between devices: none -> 3.19 us  [body(): lax.ppermute(ring[-1], 'blk', [(dev, (dev + 1) % 8) for dev in range(8)])]
    all_to_all x1, starting transfers between devices: 3.69 us -> 6.73 us  [body(): lax.all_to_all(zeta, 'blk', split_axis=1, concat_axis=0, tiled=True)]
    all_to_all x1, waiting for transfers between devices: 10.8 us -> 8.38 us  [body(): lax.all_to_all(zeta, 'blk', split_axis=1, concat_axis=0, tiled=True)]
    gather x1, local copies, waits for them, and re-layouts: 0.62 us -> 1.66 us  [body(): jnp.take_along_axis(pair_val, partner[:, :, None, None], axis=1)]
    gather x2, local copies, waits for them, and re-layouts: 1.75 us -> 0.7 us  [body(): jnp.take_along_axis(pair_con, partner[:, :, None, None], axis=1)]
  transfers between devices with their start and end apart: 5 -> 12, of which waited for: 3 -> 10; matrix products, arithmetic and copies ran while one was open for 8% -> 10% of each run, Pallas kernels for 0% -> 0%
where the time goes in v1:
time: 96.1 us; the launch traced here: 95.8 us
  waiting for transfers between devices  56.3 us (59%)
  starting transfers between devices  15.3 us (16%)
  blocking collectives  11.1 us (12%)
  local copies, waits for them, and re-layouts  6.82 us (7%)
  matrix products  4.45 us (5%)
  other arithmetic  1.56 us (2%)
    ppermute x7, waiting for transfers between devices, body(): lax.ppermute(ring[-1], 'blk', [(dev, (dev + 1) % 8) for dev in range(8)])  38.8 us
    all_to_all x1, blocking collectives, body(): lax.all_to_all(terms, ('blk', 'ga'), split_axis=0, concat_axis=0, tiled=T...  11.1 us
    all_to_all x1, waiting for transfers between devices, body(): lax.all_to_all(con_sorted, 'blk', split_axis=1, concat_axis=0, tiled=True)  8.77 us
    all_to_all x1, waiting for transfers between devices, body(): lax.all_to_all(zeta, 'blk', split_axis=1, concat_axis=0, tiled=True)  8.38 us
    all_to_all x1, starting transfers between devices, body(): lax.all_to_all(zeta, 'blk', split_axis=1, concat_axis=0, tiled=True)  6.73 us
    all_to_all x1, starting transfers between devices, body(): lax.all_to_all(con_sorted, 'blk', split_axis=1, concat_axis=0, tiled=True)  3.49 us
    ppermute x7, starting transfers between devices, body(): lax.ppermute(ring[-1], 'blk', [(dev, (dev + 1) % 8) for dev in range(8)])  3.19 us
    dot_general x4, matrix products, body(): jnp.einsum('kqxg,qgh->kqxh', held, block, preferred_element_type=jnp.floa...  3.16 us
  transfers between devices with their start and end apart: 12, of which 10 were waited for; matrix products, arithmetic and copies ran while one was open for 10% of the time, Pallas kernels for 0%

profile of v1, /device:TPU:0, one launch (start us, length us, event | category | flops | bytes accessed | tf_op | source)
XLA Modules:
  0.0 95.8 jit_solution(7993552906717018568)
XLA Ops:
  0.0 3.0 %collective-permute-start = (bf16[2,16]{1,0:T(2,128)(2,1)}, bf16[2,16]{1,0:T(2,128)(2,1)S(1)}, u32[]{:S(2)}, u32[]{:S(2)}) collective-permute-start(bf16[2,16]{1,0:T(2,128)(2,1)} %param.10), channel_id=1, source_target_pairs={{0,4},{4,8},{8,12},{12,16},{16,20},{20,24},{24,28},{28,0},{1,5},{5... | collective-permute-start | bytes 200 | tf_op jit(solution)/shard_map/ppermute | solution.py:29
  3.0 0.8 select_reduce_fusion
  3.8 0.1 reshape.97
  3.8 0.6 gather_fusion.1
  4.5 1.7 %gather_fusion.2 = bf16[32,16,512]{2,1,0:T(8,128)(2,1)S(1)} fusion(bf16[2,16,16,512]{3,2,1,0:T(8,128)(2,1)} %param.7, s32[32]{0:T(128)S(1)} %reshape.97), kind=kCustom, calls=%fused_computation.1.clone | custom fusion | bytes 1048832 | tf_op jit(solution)/shard_map/jit(take_along_axis)/gather | solution.py:39
  6.1 0.2 broadcast_select_fusion
  6.3 1.4 %collective-permute-done = bf16[2,16]{1,0:T(2,128)(2,1)S(1)} collective-permute-done((bf16[2,16]{1,0:T(2,128)(2,1)}, bf16[2,16]{1,0:T(2,128)(2,1)S(1)}, u32[]{:S(2)}, u32[]{:S(2)}) %collective-permute-start) | collective-permute-done | bytes 96 | tf_op jit(solution)/shard_map/ppermute | solution.py:29
  7.7 0.2 collective-permute-start.1
  7.9 6.1 %collective-permute-done.1 = bf16[2,16]{1,0:T(2,128)(2,1)S(1)} collective-permute-done((bf16[2,16]{1,0:T(2,128)(2,1)S(1)}, bf16[2,16]{1,0:T(2,128)(2,1)S(1)}, u32[]{:S(2)}, u32[]{:S(2)}) %collective-permute-start.1) | collective-permute-done | bytes 96 | tf_op jit(solution)/shard_map/ppermute | solution.py:29
  14.0 6.3 %collective-permute-done.2 = bf16[2,16]{1,0:T(2,128)(2,1)S(1)} collective-permute-done((bf16[2,16]{1,0:T(2,128)(2,1)S(1)}, bf16[2,16]{1,0:T(2,128)(2,1)S(1)}, u32[]{:S(2)}, u32[]{:S(2)}) %collective-permute-start.2) | collective-permute-done | bytes 96 | tf_op jit(solution)/shard_map/ppermute | solution.py:29
  20.3 6.3 %collective-permute-done.3 = bf16[2,16]{1,0:T(2,128)(2,1)S(1)} collective-permute-done((bf16[2,16]{1,0:T(2,128)(2,1)S(1)}, bf16[2,16]{1,0:T(2,128)(2,1)S(1)}, u32[]{:S(2)}, u32[]{:S(2)}) %collective-permute-start.3) | collective-permute-done | bytes 96 | tf_op jit(solution)/shard_map/ppermute | solution.py:29
  26.5 0.0 collective-permute-start.4
  26.5 6.3 %collective-permute-done.4 = bf16[2,16]{1,0:T(2,128)(2,1)S(1)} collective-permute-done((bf16[2,16]{1,0:T(2,128)(2,1)S(1)}, bf16[2,16]{1,0:T(2,128)(2,1)S(1)}, u32[]{:S(2)}, u32[]{:S(2)}) %collective-permute-start.4) | collective-permute-done | bytes 96 | tf_op jit(solution)/shard_map/ppermute | solution.py:29
  32.8 0.0 collective-permute-start.5
  32.8 6.3 %collective-permute-done.5 = bf16[2,16]{1,0:T(2,128)(2,1)S(1)} collective-permute-done((bf16[2,16]{1,0:T(2,128)(2,1)S(1)}, bf16[2,16]{1,0:T(2,128)(2,1)S(1)}, u32[]{:S(2)}, u32[]{:S(2)}) %collective-permute-start.5) | collective-permute-done | bytes 96 | tf_op jit(solution)/shard_map/ppermute | solution.py:29
  39.1 0.0 collective-permute-start.6
  39.1 6.3 %collective-permute-done.6 = bf16[2,16]{1,0:T(2,128)(2,1)S(1)} collective-permute-done((bf16[2,16]{1,0:T(2,128)(2,1)S(1)}, bf16[2,16]{1,0:T(2,128)(2,1)S(1)}, u32[]{:S(2)}, u32[]{:S(2)}) %collective-permute-start.6) | collective-permute-done | bytes 96 | tf_op jit(solution)/shard_map/ppermute | solution.py:29
  45.3 0.1 concatenate.6
  45.5 0.8 copy.96
  46.3 3.5 %all-to-all-start.1 = ((bf16[2,16,16,512]{3,2,0,1:T(8,128)(2,1)}), bf16[2,16,16,512]{3,2,0,1:T(8,128)(2,1)S(1)}, u32[]{:S(2)}, u32[]{:S(2)}) async-start(bf16[2,16,16,512]{3,2,0,1:T(8,128)(2,1)} %copy.96), calls=%async_computation.1 | async-start | bytes 1048576 | tf_op jit(solution)/shard_map/all_to_all | solution.py:38
  49.8 0.1 reshape.78
  49.9 0.1 reshape.57
  50.0 0.6 gather_fusion
  50.6 0.1 copy.90
  50.7 0.1 reshape.56
  50.8 0.1 copy.107
  50.9 0.4 fusion.2
  51.4 0.1 reshape.58
  51.5 0.8 copy.92
  52.3 8.8 %all-to-all-done.1 = bf16[2,16,16,512]{3,2,0,1:T(8,128)(2,1)S(1)} async-done(((bf16[2,16,16,512]{3,2,0,1:T(8,128)(2,1)}), bf16[2,16,16,512]{3,2,0,1:T(8,128)(2,1)S(1)}, u32[]{:S(2)}, u32[]{:S(2)}) %all-to-all-start.1) | async-done | bytes 524320 | tf_op jit(solution)/shard_map/all_to_all | solution.py:38
  61.1 6.7 %all-to-all-start = ((bf16[2,16,16,512]{3,2,0,1:T(8,128)(2,1)}), bf16[2,16,16,512]{3,2,0,1:T(8,128)(2,1)S(1)}, u32[]{:S(2)}, u32[]{:S(2)}) async-start(bf16[2,16,16,512]{3,2,0,1:T(8,128)(2,1)} %copy.92), calls=%async_computation | async-start | bytes 1048576 | tf_op jit(solution)/shard_map/all_to_all | solution.py:48
  67.9 1.9 %collective-permute-start.8 = (bf16[16,2,16,512]{3,2,0,1:T(8,128)(2,1)S(1)}, bf16[16,2,16,512]{3,2,0,1:T(8,128)(2,1)S(1)}, u32[]{:S(2)}, u32[]{:S(2)}) collective-permute-start(bf16[16,2,16,512]{3,2,0,1:T(8,128)(2,1)S(1)} %bitcast.89), channel_id=1, source_target_pairs={{0,2},{1,3},{2,0},{3,1},{4,6},{5,7},{6,4},{7,5},{8,10},{9,11},{10,... | collective-permute-start | bytes 1572872 | tf_op jit(solution)/shard_map/ppermute | solution.py:18
  69.7 8.4 %all-to-all-done = bf16[2,16,16,512]{3,2,0,1:T(8,128)(2,1)S(1)} async-done(((bf16[2,16,16,512]{3,2,0,1:T(8,128)(2,1)}), bf16[2,16,16,512]{3,2,0,1:T(8,128)(2,1)S(1)}, u32[]{:S(2)}, u32[]{:S(2)}) %all-to-all-start) | async-done | bytes 524320 | tf_op jit(solution)/shard_map/all_to_all | solution.py:48
  78.1 0.5 copy.94
  78.6 0.0 copy-start.2
  78.7 1.8 %fusion.6 = f32[2,512,16,16]{1,3,2,0:T(8,128)S(1)} fusion(bf16[16,2,16,512]{3,2,0,1:T(8,128)(2,1)S(1)} %bitcast.91, bf16[2,4,512,512]{3,2,1,0:T(8,128)(2,1)} %bitcast.95, s32[]{:T(128)S(6)} %select_n.45), kind=kOutput, calls=%fused_computation.14 | convolution fusion | flops 268435456 | bytes 2621444 | tf_op jit(solution)/shard_map/kqxg,qgh->kqxh/dot_general | solution.py:54
  80.5 0.1 collective-permute-start.9
  80.6 0.0 collective-permute-done.7
  80.6 0.6 copy-done.2
  81.2 0.4 convolution_add_fusion.2
  81.6 0.5 convolution_add_fusion.1
  82.1 0.4 collective-permute-done.9
  82.5 0.4 fusion.1
  82.9 0.1 reshape.61
  83.0 0.9 convolution_bitcast_fusion
  83.9 0.1 broadcast_in_dim.22
  84.1 11.1 %all_to_all.38 = f32[32,2,16]{2,1,0:T(2,128)S(1)} all-to-all(f32[32,2,16]{2,1,0:T(2,128)S(1)} %copy.105), channel_id=1, replica_groups=mesh['blk'=8,'ga'=4] {'blk','ga'}, dimensions={0} | all-to-all | bytes 8192 | tf_op jit(solution)/shard_map/all_to_all | solution.py:64
  95.2 0.6 broadcast_multiply_fusion
  (17 shorter events, 0.2 us)
Async XLA Ops:
  0.0 3.8 %copy-start = (bf16[2,16,16,512]{3,2,1,0:T(8,128)(2,1)S(1)}, bf16[2,16,16,512]{3,2,1,0:T(8,128)(2,1)}, u32[]{:S(2)}) copy-start(bf16[2,16,16,512]{3,2,1,0:T(8,128)(2,1)} %param.8) | copy-start | bytes 1572868
  0.0 45.3 %copy-start.1 = (bf16[2,16]{1,0:T(2,128)(2,1)S(1)}, bf16[2,16]{1,0:T(2,128)(2,1)}, u32[]{:S(2)}) copy-start(bf16[2,16]{1,0:T(2,128)(2,1)} %param.10) | copy-start | bytes 196
  0.0 7.7 %collective-permute-start = (bf16[2,16]{1,0:T(2,128)(2,1)}, bf16[2,16]{1,0:T(2,128)(2,1)S(1)}, u32[]{:S(2)}, u32[]{:S(2)}) collective-permute-start(bf16[2,16]{1,0:T(2,128)(2,1)} %param.10), channel_id=1, source_target_pairs={{0,4},{4,8},{8,12},{12,16},{16,20},{20,24},{24,28},{28,0},{1,5},{5... | collective-permute-start | bytes 200 | tf_op jit(solution)/shard_map/ppermute | solution.py:29
  7.7 6.3 %collective-permute-start.1 = (bf16[2,16]{1,0:T(2,128)(2,1)S(1)}, bf16[2,16]{1,0:T(2,128)(2,1)S(1)}, u32[]{:S(2)}, u32[]{:S(2)}) collective-permute-start(bf16[2,16]{1,0:T(2,128)(2,1)S(1)} %collective-permute-done), channel_id=1, source_target_pairs={{0,4},{4,8},{8,12},{12,16},{16,20},{20,24},{24,28},{28,0},{1,5},{5... | collective-permute-start | bytes 200 | tf_op jit(solution)/shard_map/ppermute | solution.py:29
  14.0 6.3 %collective-permute-start.2 = (bf16[2,16]{1,0:T(2,128)(2,1)S(1)}, bf16[2,16]{1,0:T(2,128)(2,1)S(1)}, u32[]{:S(2)}, u32[]{:S(2)}) collective-permute-start(bf16[2,16]{1,0:T(2,128)(2,1)S(1)} %collective-permute-done.1), channel_id=1, source_target_pairs={{0,4},{4,8},{8,12},{12,16},{16,20},{20,24},{24,28},{28,0},{1,5},{5... | collective-permute-start | bytes 200 | tf_op jit(solution)/shard_map/ppermute | solution.py:29
  20.3 6.3 %collective-permute-start.3 = (bf16[2,16]{1,0:T(2,128)(2,1)S(1)}, bf16[2,16]{1,0:T(2,128)(2,1)S(1)}, u32[]{:S(2)}, u32[]{:S(2)}) collective-permute-start(bf16[2,16]{1,0:T(2,128)(2,1)S(1)} %collective-permute-done.2), channel_id=1, source_target_pairs={{0,4},{4,8},{8,12},{12,16},{16,20},{20,24},{24,28},{28,0},{1,5},{5... | collective-permute-start | bytes 200 | tf_op jit(solution)/shard_map/ppermute | solution.py:29
  26.5 6.3 %collective-permute-start.4 = (bf16[2,16]{1,0:T(2,128)(2,1)S(1)}, bf16[2,16]{1,0:T(2,128)(2,1)S(1)}, u32[]{:S(2)}, u32[]{:S(2)}) collective-permute-start(bf16[2,16]{1,0:T(2,128)(2,1)S(1)} %collective-permute-done.3), channel_id=1, source_target_pairs={{0,4},{4,8},{8,12},{12,16},{16,20},{20,24},{24,28},{28,0},{1,5},{5... | collective-permute-start | bytes 200 | tf_op jit(solution)/shard_map/ppermute | solution.py:29
  32.8 6.3 %collective-permute-start.5 = (bf16[2,16]{1,0:T(2,128)(2,1)S(1)}, bf16[2,16]{1,0:T(2,128)(2,1)S(1)}, u32[]{:S(2)}, u32[]{:S(2)}) collective-permute-start(bf16[2,16]{1,0:T(2,128)(2,1)S(1)} %collective-permute-done.4), channel_id=1, source_target_pairs={{0,4},{4,8},{8,12},{12,16},{16,20},{20,24},{24,28},{28,0},{1,5},{5... | collective-permute-start | bytes 200 | tf_op jit(solution)/shard_map/ppermute | solution.py:29
  39.1 6.3 %collective-permute-start.6 = (bf16[2,16]{1,0:T(2,128)(2,1)S(1)}, bf16[2,16]{1,0:T(2,128)(2,1)S(1)}, u32[]{:S(2)}, u32[]{:S(2)}) collective-permute-start(bf16[2,16]{1,0:T(2,128)(2,1)S(1)} %collective-permute-done.5), channel_id=1, source_target_pairs={{0,4},{4,8},{8,12},{12,16},{16,20},{20,24},{24,28},{28,0},{1,5},{5... | collective-permute-start | bytes 200 | tf_op jit(solution)/shard_map/ppermute | solution.py:29
  46.3 14.8 %all-to-all-start.1 = ((bf16[2,16,16,512]{3,2,0,1:T(8,128)(2,1)}), bf16[2,16,16,512]{3,2,0,1:T(8,128)(2,1)S(1)}, u32[]{:S(2)}, u32[]{:S(2)}) async-start(bf16[2,16,16,512]{3,2,0,1:T(8,128)(2,1)} %copy.96), calls=%async_computation.1 | async-start | bytes 1048576 | tf_op jit(solution)/shard_map/all_to_all | solution.py:38
  61.1 17.0 %all-to-all-start = ((bf16[2,16,16,512]{3,2,0,1:T(8,128)(2,1)}), bf16[2,16,16,512]{3,2,0,1:T(8,128)(2,1)S(1)}, u32[]{:S(2)}, u32[]{:S(2)}) async-start(bf16[2,16,16,512]{3,2,0,1:T(8,128)(2,1)} %copy.92), calls=%async_computation | async-start | bytes 1048576 | tf_op jit(solution)/shard_map/all_to_all | solution.py:48
  67.9 12.6 %collective-permute-start.8 = (bf16[16,2,16,512]{3,2,0,1:T(8,128)(2,1)S(1)}, bf16[16,2,16,512]{3,2,0,1:T(8,128)(2,1)S(1)}, u32[]{:S(2)}, u32[]{:S(2)}) collective-permute-start(bf16[16,2,16,512]{3,2,0,1:T(8,128)(2,1)S(1)} %bitcast.89), channel_id=1, source_target_pairs={{0,2},{1,3},{2,0},{3,1},{4,6},{5,7},{6,4},{7,5},{8,10},{9,11},{10,... | collective-permute-start | bytes 1572872 | tf_op jit(solution)/shard_map/ppermute | solution.py:18
  69.7 10.9 %collective-permute-start.7 = (bf16[16,2,16,512]{3,2,0,1:T(8,128)(2,1)S(1)}, bf16[16,2,16,512]{3,2,0,1:T(8,128)(2,1)S(1)}, u32[]{:S(2)}, u32[]{:S(2)}) collective-permute-start(bf16[16,2,16,512]{3,2,0,1:T(8,128)(2,1)S(1)} %bitcast.90), channel_id=1, source_target_pairs={{0,1},{1,0},{2,3},{3,2},{4,5},{5,4},{6,7},{7,6},{8,9},{9,8},{10,11... | collective-permute-start | bytes 1572872 | tf_op jit(solution)/shard_map/ppermute | solution.py:18
  78.6 2.5 %copy-start.2 = (bf16[2,2048,512]{2,1,0:T(8,128)(2,1)S(1)}, bf16[2,2048,512]{2,1,0:T(8,128)(2,1)}, u32[]{:S(2)}) copy-start(bf16[2,2048,512]{2,1,0:T(8,128)(2,1)} %param.9) | copy-start | bytes 12582916
  80.5 2.0 %collective-permute-start.9 = (bf16[16,2,16,512]{3,2,0,1:T(8,128)(2,1)S(1)}, bf16[16,2,16,512]{3,2,0,1:T(8,128)(2,1)S(1)}, u32[]{:S(2)}, u32[]{:S(2)}) collective-permute-start(bf16[16,2,16,512]{3,2,0,1:T(8,128)(2,1)S(1)} %collective-permute-done.8), channel_id=1, source_target_pairs={{0,1},{1,0},{2,3},{3,2},{4,5},{5,4},{6,7},{7,6},{8,9},{9,8},{10,11... | collective-permute-start | bytes 1572872 | tf_op jit(solution)/shard_map/ppermute | solution.py:18
